TPU v7x, 128 devices: a whole 4x4x4 slice. The times are simulated.
128 devices in a mesh: grp: 4 (over z), seq: 32 (over x, y, core).
Axes of the slice: x: 4, y: 4, z: 4, core: 2. Of those that a mesh axis runs over, the one named last changes fastest.
Arguments:
- latent: bfloat16 [4, 4096, 32, 256], P('grp', 'seq'), may hold values from -6 to 6
- up_key: bfloat16 [4, 128, 256], replicated, may hold values from -0.5 to 0.5
- up_value: bfloat16 [4, 128, 256], replicated, may hold values from -0.5 to 0.5
- queries: bfloat16 [8, 64, 128], replicated, may hold values from -240 to 240, as said below
- lengths: int32 [8], replicated, may hold values from 1 to 16384
- block_dest: int32 [4096], replicated, may hold values from 0 to 127, as said below
Outputs:
- decode_latent: bfloat16 [128, 4, 32, 32, 256], P(('grp', 'seq'))
- attended: float32 [8, 8192], replicated
Inputs may be any that keep to these rules, and one draw needn't show every extreme that they name: `block_dest`: each aligned run of 128 entries (the blocks of one seq index in the prefill layout) names every decode device exactly once. `queries`: the new token's query entries, real-valued.
All inputs are finite; a program needn't handle non-finite values.
Results may differ from a plain program's by a relative error of at most 0.001.
Values may be sent and summed in bfloat16 or wider, within the bound.
A program may use at most 64 MiB of HBM per device.

v0:
```python
import jax
import jax.numpy as jnp
from jax import lax
from jax.sharding import Mesh
from jax.sharding import PartitionSpec as P

SEQ = ("seq_0", "seq_1", "seq_2")
GRP_SEQ = ("grp", "seq_0", "seq_1", "seq_2")


def all_in_one(x, axis):
    leaves = jax.tree.leaves(x)
    turns = sorted(range(len(leaves)), key=lambda k: -leaves[k].size)
    width = (1, *leaves[turns[0]].shape)[-1]
    lines = [
        jnp.pad(leaves[k].reshape(-1), (0, -leaves[k].size % width)).reshape(-1, width)
        for k in turns
    ]
    both, at, found = (lax.all_gather(jnp.concatenate(lines), axis), 0, {})
    for k, line in zip(turns, lines):
        slab = both[:, at : at + len(line)].reshape(len(both), -1)
        found[k] = slab[:, : leaves[k].size].reshape(-1, *leaves[k].shape)
        at += len(line)
    numbers = iter(range(len(leaves)))
    return jax.tree.map(lambda _: found[next(numbers)], x)


def joined_all(x, axes, combine):
    for axis in axes:
        pieces = all_in_one(x, axis)
        x = jax.tree.map(lambda part: part[0], pieces)
        for k in range(1, lax.axis_size(axis)):
            x = combine(x, jax.tree.map(lambda part: part[k], pieces))
    return x


def combine(first, second):
    largest = jnp.maximum(first[0], second[0])
    factor_a = jnp.exp(first[0] - largest)
    factor_b = jnp.exp(second[0] - largest)
    totals = first[1] * factor_a + second[1] * factor_b
    accum = first[2] * factor_a[..., None] + second[2] * factor_b[..., None]
    return (largest, totals, accum)


def slot_info(global_ids, lengths, block_len, blk_seq, batch):
    seq_ids = global_ids // blk_seq
    starts = global_ids % blk_seq * block_len
    positions = starts[:, None] + jnp.arange(block_len, dtype=jnp.int32)[None, :]
    seq_hot = (seq_ids[:, None] == jnp.arange(batch, dtype=jnp.int32)[None, :]).astype(jnp.int32)
    slot_len = jnp.sum(seq_hot * lengths[None, :], axis=1)
    live = positions < slot_len[:, None]
    return (seq_hot, live)


def partials(cache, key_map, value_map, slot_query, live, seq_hot):
    rank = cache.shape[3] // 2
    head_dim = slot_query.shape[-1]
    scale = 1.0 / float(head_dim) ** 0.5
    highest = lax.Precision.HIGHEST
    key_lat = cache[..., :rank]
    value_lat = cache[..., rank:]
    keys = jnp.einsum("gstr,grkd->gstkd", key_lat, key_map, preferred_element_type=jnp.float32)
    scores = (
        jnp.einsum("gstkd,sgkjd->gskjt", keys, slot_query.astype(jnp.float32), precision=highest)
        * scale
    )
    live_wide = live[None, :, None, None, :]
    scores = jnp.where(live_wide, scores, -1e30)
    slot_max = jnp.max(scores, axis=-1)
    weights = jnp.where(live_wide, jnp.exp(scores - slot_max[..., None]), 0.0)
    slot_tot = jnp.sum(weights, axis=-1)
    values = jnp.einsum(
        "gstr,grkd->gstkd", value_lat, value_map, preferred_element_type=jnp.float32
    )
    slot_acc = jnp.einsum("gskjt,gstkd->gskjd", weights, values, precision=highest)
    hot_bool = seq_hot > 0
    hot_float = seq_hot.astype(jnp.float32)
    spread = jnp.where(hot_bool[None, :, None, None, :], slot_max[..., None], -1e30)
    seq_max = jnp.max(spread, axis=1)
    slot_seq_max = jnp.sum(
        jnp.where(hot_bool[None, :, None, None, :], seq_max[:, None], 0.0), axis=-1
    )
    factor = jnp.exp(slot_max - slot_seq_max)
    totals = jnp.einsum("gskj,sb->gkjb", slot_tot * factor, hot_float, precision=highest)
    accum = jnp.einsum(
        "gskjd,sb->gkjbd", slot_acc * factor[..., None], hot_float, precision=highest
    )
    return (seq_max, totals, accum)


def body(latent, up_key, up_value, queries, lengths, block_dest):
    groups = up_key.shape[0]
    dests = latent.shape[1]
    block_len = latent.shape[2]
    rank = latent.shape[3] // 2
    shards = block_dest.shape[0] // dests
    batch = queries.shape[0]
    q_heads = queries.shape[1]
    head_dim = queries.shape[2]
    per_group = up_key.shape[2] // head_dim
    per_kv = q_heads // (groups * per_group)
    blk_seq = block_dest.shape[0] // batch
    own_shard = lax.axis_index(SEQ)
    own_dests = lax.dynamic_slice_in_dim(block_dest, own_shard * dests, dests)
    source_order = (
        jnp.zeros((dests,), jnp.int32).at[own_dests].set(jnp.arange(dests, dtype=jnp.int32))
    )
    outgoing = latent[0][source_order]
    received = lax.all_to_all(outgoing, GRP_SEQ, split_axis=0, concat_axis=0, tiled=True)
    received = received.reshape(groups, shards, block_len, 2 * rank)
    decode_latent = received[None]
    key_map = up_key.reshape(groups, rank, per_group, head_dim)
    value_map = up_value.reshape(groups, rank, per_group, head_dim)
    query_rows = queries.reshape(batch, q_heads * head_dim)
    own_group = lax.axis_index("grp")
    slots = latent.shape[1]
    global_ids = own_shard * slots + jnp.arange(slots, dtype=jnp.int32)
    seq_hot, live = slot_info(global_ids, lengths, block_len, blk_seq, batch)
    picked = jnp.dot(seq_hot.astype(jnp.bfloat16), query_rows, preferred_element_type=jnp.float32)
    slot_query = picked.astype(jnp.bfloat16).reshape(slots, groups, per_group, per_kv, head_dim)
    group_query = lax.dynamic_slice_in_dim(slot_query, own_group, 1, 1)
    group_key = lax.dynamic_slice_in_dim(key_map, own_group, 1, 0)
    group_value = lax.dynamic_slice_in_dim(value_map, own_group, 1, 0)
    local = partials(latent, group_key, group_value, group_query, live, seq_hot)
    merged = joined_all(local, SEQ, combine)
    part_result = merged[2] / merged[1][..., None]
    result = lax.all_gather(part_result, "grp", axis=0, tiled=True)
    attended = jnp.transpose(result, (3, 0, 1, 2, 4)).reshape(batch, q_heads * head_dim)
    return (decode_latent, attended)


def solution(mesh):
    finer = Mesh(
        mesh.devices.reshape(mesh.shape["grp"], 4, 4, 2), ("grp", "seq_0", "seq_1", "seq_2")
    )
    in_specs = (P("grp", SEQ, None, None), P(), P(), P(), P(), P())
    out_specs = (P(GRP_SEQ, None, None, None, None), P())
    return jax.shard_map(body, mesh=finer, in_specs=in_specs, out_specs=out_specs, check_vma=False)
```

profile of v0, /device:TPU:0, one launch (start us, length us, event | category | flops | bytes accessed | tf_op | source)
XLA Modules:
  0.0 82.2 jit_solution(2277621008148799493)
XLA Ops:
  0.6 0.8 compare_select_fusion.1
  1.4 1.0 %scatter_custom_fusion = s32[128]{0:T(128)S(1)} fusion(s32[128]{0:T(128)S(1)} %compare_select_fusion.1, s32[128]{0:T(128)S(1)} %iota.27, s32[]{:T(128)} %constant.26.clone.1), kind=kCustom, calls=%fused_computation.172 | custom fusion | bytes 516 | tf_op jit(solution)/shard_map/scatter | solution.py:107
  2.4 3.6 %gather_fusion = bf16[128,32,256]{2,1,0:T(8,128)(2,1)} fusion(bf16[128,32,256]{2,1,0:T(8,128)(2,1)} %bitcast.358, s32[1024]{0:T(1024)S(1)} %pad_clamp_fusion), kind=kCustom, calls=%fused_computation | custom fusion | bytes 4194816 | tf_op jit(solution)/shard_map/gather | solution.py:109
  6.0 11.7 %all-to-all-start = ((bf16[128,32,256]{2,1,0:T(8,128)(2,1)}), bf16[128,32,256]{2,1,0:T(8,128)(2,1)}, u32[]{:S(2)}, u32[]{:S(2)}) async-start(bf16[128,32,256]{2,1,0:T(8,128)(2,1)} %gather_fusion), calls=%async_computation | async-start | bytes 4194304 | tf_op jit(solution)/shard_map/all_to_all | solution.py:110
  18.0 0.1 constant_dynamic-slice_fusion
  18.1 0.7 fusion.14
  18.8 0.2 copy-done.3
  19.0 0.7 fusion.4
  19.8 0.6 copy.35
  20.4 0.1 add_compare_fusion
  20.5 3.6 %fusion.102 = (f32[128,2,8]{2,1,0:T(2,128)S(1)}, f32[128,2,8,32]{3,2,1,0:T(8,128)S(1)}) fusion(f32[2,128,128,32]{1,3,0,2:T(8,128)S(1)} %fusion.14, bf16[128,4,2,8,128]{4,3,2,1,0:T(8,128)(2,1)S(1)} %bitcast.359, s32[]{:T(128)S(6)} %select_n.72, pred[128,32]{1,0:T(8,128)(4,1)S(1)} %add_compare_fusion), kind=kOutput, calls=%fused_computation.176 | convolution fusion | flops 100857856 | bytes 5005316 | tf_op jit(solution)/shard_map/gstkd,sgkjd->gskjt/dot_general | solution.py:65
  24.2 0.1 select_reduce_fusion.1
  24.3 0.1 select_reduce_fusion
  24.4 0.1 reshape.1166
  24.5 0.1 copy.26
  24.7 0.7 convolution_bitcast_fusion
  25.4 0.8 fusion.21
  26.2 3.7 %fusion.5 = f32[128,2,8,128]{3,2,1,0:T(8,128)S(1)} fusion(f32[128,32,2,128]{3,1,0,2:T(8,128)S(1)} %convolution_bitcast_fusion, f32[128,2,8,32]{3,2,1,0:T(8,128)S(1)} %get-tuple-element.30, f32[128,2,8]{2,1,0:T(2,128)S(1)} %copy.26, f32[128,2,8]{2,1,0:T(2,128)S(1)} %get-tuple-element.29, pred[128,32]{1,0:T(8,128)(4,1)S(1)} %add_compare_fusion), kind=kOutput, calls=%fused_computation.9 | convolution fusion | flops 101056512 | bytes 5525504 | tf_op jit(solution)/shard_map/gskjt,gstkd->gskjd/dot_general | solution.py:76
  29.9 0.9 %fusion.17 = f32[8,2,8,128]{3,0,2,1:T(8,128)S(1)} fusion(f32[128,2,8,128]{3,2,1,0:T(8,128)S(1)} %fusion.5, s32[128]{0:T(128)S(1)} %get-tuple-element.31), kind=kOutput, calls=%fused_computation.15 | convolution fusion | flops 25168896 | bytes 1114624 | tf_op jit(solution)/shard_map/gskjd,sb->gkjbd/dot_general | solution.py:86
  30.8 0.1 fusion.49
  30.9 0.1 reshape.1167
  31.1 18.3 %all-gather.3 = f32[4,130,128]{2,1,0:T(8,128)S(1)} all-gather(f32[1,130,128]{2,1,0:T(8,128)S(1)} %maximum_bitcast_fusion), channel_id=2, replica_groups=mesh['grp'=4,'seq_0'=4,'seq_1'=4,'seq_2'=2] {'seq_0'}, dimensions={0}, use_global_device_ids=true | all-gather | bytes 332800 | tf_op jit(solution)/shard_map/all_gather | solution.py:19
  49.4 0.2 fusion.39
  49.6 12.7 %all-gather.4 = f32[4,130,128]{2,1,0:T(8,128)S(1)} all-gather(f32[1,130,128]{2,1,0:T(8,128)S(1)} %maximum_bitcast_fusion.1), channel_id=3, replica_groups=mesh['grp'=4,'seq_0'=4,'seq_1'=4,'seq_2'=2] {'seq_1'}, dimensions={0}, use_global_device_ids=true | all-gather | bytes 332800 | tf_op jit(solution)/shard_map/all_gather | solution.py:19
  62.4 0.2 fusion.30
  62.6 1.9 %all-gather.5 = f32[2,130,128]{2,1,0:T(8,128)S(1)} all-gather(f32[1,130,128]{2,1,0:T(8,128)S(1)} %maximum_bitcast_fusion.2), channel_id=4, replica_groups=mesh['grp'=4,'seq_0'=4,'seq_1'=4,'seq_2'=2] {'seq_2'}, dimensions={0}, use_global_device_ids=true | all-gather | bytes 199680 | tf_op jit(solution)/shard_map/all_gather | solution.py:19
  64.7 0.1 squeeze.146
  64.8 0.1 squeeze.147
  64.9 0.1 add_divide_fusion
  65.0 13.4 %all_gather.27 = f32[4,2,8,8,128]{4,3,2,1,0:T(8,128)S(1)} all-gather(f32[1,2,8,8,128]{4,3,2,1,0:T(8,128)S(1)} %add_divide_fusion), channel_id=1, replica_groups=mesh['grp'=4,'seq_0'=4,'seq_1'=4,'seq_2'=2] {'grp'}, dimensions={0}, use_global_device_ids=true | all-gather | bytes 327680 | tf_op jit(solution)/shard_map/all_gather | solution.py:128
  78.4 3.1 %copy.52 = bf16[1,4,32,32,256]{4,3,2,1,0:T(8,128)(2,1)} copy(bf16[1,4,32,32,256]{4,3,2,1,0:T(8,128)(2,1)} %bitcast.1) | data formatting | bytes 4194304
  81.5 0.7 copy.53
  (35 shorter events, 0.7 us)
Async XLA Ops:
  6.0 11.8 %copy-start.4 = (s32[8]{0:T(128)S(1)}, s32[8]{0:T(128)}, u32[]{:S(2)}) copy-start(s32[8]{0:T(128)} %param.10) | copy-start | bytes 100
  6.0 11.9 %copy-start.1 = (bf16[4,128,256]{2,1,0:T(8,128)(2,1)S(1)}, bf16[4,128,256]{2,1,0:T(8,128)(2,1)}, u32[]{:S(2)}) copy-start(bf16[4,128,256]{2,1,0:T(8,128)(2,1)} %param.7) | copy-start | bytes 786436
  6.0 11.9 %copy-start.2 = (bf16[4,128,256]{2,1,0:T(8,128)(2,1)S(1)}, bf16[4,128,256]{2,1,0:T(8,128)(2,1)}, u32[]{:S(2)}) copy-start(bf16[4,128,256]{2,1,0:T(8,128)(2,1)} %param.8) | copy-start | bytes 786436
  6.0 12.1 %copy-start = (bf16[1,128,32,256]{3,2,1,0:T(8,128)(2,1)S(1)}, bf16[1,128,32,256]{3,2,1,0:T(8,128)(2,1)}, u32[]{:S(2)}) copy-start(bf16[1,128,32,256]{3,2,1,0:T(8,128)(2,1)} %param.6) | copy-start | bytes 6291460
  6.0 72.4 %all-to-all-start = ((bf16[128,32,256]{2,1,0:T(8,128)(2,1)}), bf16[128,32,256]{2,1,0:T(8,128)(2,1)}, u32[]{:S(2)}, u32[]{:S(2)}) async-start(bf16[128,32,256]{2,1,0:T(8,128)(2,1)} %gather_fusion), calls=%async_computation | async-start | bytes 4194304 | tf_op jit(solution)/shard_map/all_to_all | solution.py:110
  18.1 0.9 %copy-start.3 = (bf16[8,64,128]{2,1,0:T(8,128)(2,1)S(1)}, bf16[8,64,128]{2,1,0:T(8,128)(2,1)}, u32[]{:S(2)}) copy-start(bf16[8,64,128]{2,1,0:T(8,128)(2,1)} %param.9) | copy-start | bytes 393220
where the time goes:
time: 82.5 us; the launch traced here: 82.2 us
  blocking collectives  46.3 us (56%)
  starting transfers between devices  11.7 us (14%)
  matrix products  10.4 us (13%)
  local copies, waits for them, and re-layouts  10.2 us (12%)
  other arithmetic  2.58 us (3%)
  between operations  0.89 us (1%)
    all_gather x3, blocking collectives, all_in_one(): both, at, found = (lax.all_gather(jnp.concatenate(lines), axis), 0, {})  32.9 us
    all_gather x1, blocking collectives, body(): result = lax.all_gather(part_result, 'grp', axis=0, tiled=True)  13.4 us
    all_to_all x1, starting transfers between devices, body(): lax.all_to_all(outgoing, GRP_SEQ, split_axis=0, concat_axis=0, tiled=True)  11.7 us
    unnamed x13, local copies, waits for them, and re-layouts  4.61 us
    dot_general x1, matrix products, partials(): jnp.einsum('gskjt,gstkd->gskjd', weights, values, precision=highest)  3.68 us
    dot_general x1, matrix products, partials(): jnp.einsum('gstkd,sgkjd->gskjt', keys, slot_query.astype(jnp.float32), pr...  3.63 us
    gather x1, local copies, waits for them, and re-layouts, body(): outgoing = latent[0][source_order]  3.59 us
  transfers between devices with their start and end apart: 1, of which 0 were waited for; matrix products, arithmetic and copies ran while one was open for 17% of the time, Pallas kernels for 0%

commit v1 on v0

--- a/solution.py
+++ b/solution.py
@@ -125,7 +125,9 @@
     local = partials(latent, group_key, group_value, group_query, live, seq_hot)
     merged = joined_all(local, SEQ, combine)
     part_result = merged[2] / merged[1][..., None]
-    result = lax.all_gather(part_result, "grp", axis=0, tiled=True)
+    result = jnp.concatenate(
+        lax.all_to_all(jnp.stack([part_result] * lax.axis_size("grp")), "grp", 0, 0), axis=0
+    )
     attended = jnp.transpose(result, (3, 0, 1, 2, 4)).reshape(batch, q_heads * head_dim)
     return (decode_latent, attended)
 

time: 82.5 us -> 103 us (1.25)
  waiting for transfers between devices: 0.01 us -> 33.6 us
  blocking collectives: 46.3 us -> 27.6 us
  matrix products: 10.4 us -> 13 us
  other arithmetic: 2.58 us -> 3.88 us
    all_to_all x1, waiting for transfers between devices: 0.01 us -> 30.3 us  [body(): lax.all_to_all(outgoing, GRP_SEQ, split_axis=0, concat_axis=0, tiled=True)]
    all_gather x1 -> x0, blocking collectives: 13.4 us -> none  [body(): result = lax.all_gather(part_result, 'grp', axis=0, tiled=True)]
    all_gather x3, blocking collectives: 32.9 us -> 27.6 us  [all_in_one(): both, at, found = (lax.all_gather(jnp.concatenate(lines), axis), 0, {})]
    all_to_all x0 -> x1, starting transfers between devices: none -> 5.3 us  [body(): lax.all_to_all(jnp.stack([part_result] * lax.axis_size('grp')), 'grp', 0, 0)]
    all_to_all x1, starting transfers between devices: 11.7 us -> 6.85 us  [body(): lax.all_to_all(outgoing, GRP_SEQ, split_axis=0, concat_axis=0, tiled=True)]
    all_to_all x0 -> x1, waiting for transfers between devices: none -> 3.22 us  [body(): lax.all_to_all(jnp.stack([part_result] * lax.axis_size('grp')), 'grp', 0, 0)]
    gather x1, local copies, waits for them, and re-layouts: 3.59 us -> 2 us  [body(): outgoing = latent[0][source_order]]
    unnamed x13 -> x11, local copies, waits for them, and re-layouts: 4.61 us -> 3.96 us
  transfers between devices with their start and end apart: 1 -> 2, of which waited for: 0 -> 2; matrix products, arithmetic and copies ran while one was open for 17% -> 4% of each run, Pallas kernels for 0% -> 0%
where the time goes in v1:
time: 103 us; the launch traced here: 102 us
  waiting for transfers between devices  33.6 us (33%)
  blocking collectives  27.6 us (27%)
  matrix products  13 us (13%)
  starting transfers between devices  12.2 us (12%)
  local copies, waits for them, and re-layouts  11.1 us (11%)
  other arithmetic  3.88 us (4%)
    all_to_all x1, waiting for transfers between devices, body(): lax.all_to_all(outgoing, GRP_SEQ, split_axis=0, concat_axis=0, tiled=True)  30.3 us
    all_gather x3, blocking collectives, all_in_one(): both, at, found = (lax.all_gather(jnp.concatenate(lines), axis), 0, {})  27.6 us
    all_to_all x1, starting transfers between devices, body(): lax.all_to_all(outgoing, GRP_SEQ, split_axis=0, concat_axis=0, tiled=True)  6.85 us
    all_to_all x1, starting transfers between devices, body(): lax.all_to_all(jnp.stack([part_result] * lax.axis_size('grp')), 'grp', 0, 0)  5.3 us
    dot_general x1, matrix products, partials(): jnp.einsum('gstkd,sgkjd->gskjt', keys, slot_query.astype(jnp.float32), pr...  4.59 us
    unnamed x11, local copies, waits for them, and re-layouts  3.96 us
    dot_general x1, matrix products, partials(): jnp.einsum('gskjt,gstkd->gskjd', weights, values, precision=highest)  3.68 us
    all_to_all x1, waiting for transfers between devices, body(): lax.all_to_all(jnp.stack([part_result] * lax.axis_size('grp')), 'grp', 0, 0)  3.22 us
  transfers between devices with their start and end apart: 2, of which 2 were waited for; matrix products, arithmetic and copies ran while one was open for 4% of the time, Pallas kernels for 0%

profile of v1, /device:TPU:0, one launch (start us, length us, event | category | flops | bytes accessed | tf_op | source)
XLA Modules:
  0.0 102.2 jit_solution(5024506107533336421)
XLA Ops:
  0.7 0.7 select_reduce_fusion.2
  1.4 1.0 reshape.1154
  2.4 1.0 reshape.1157
  3.5 1.7 %fusion.4 = bf16[16,8,64,128]{3,1,2,0:T(8,128)(2,1)S(1)} fusion(bf16[1,8,64,128]{3,2,1,0:T(8,128)(2,1)} %bitcast.367, s32[128]{0:T(128)S(1)} %get-tuple-element.31), kind=kOutput, calls=%fused_computation.8 | convolution fusion | flops 17828864 | bytes 2228736 | tf_op jit(solution)/shard_map/dot_general | solution.py:120
  5.1 1.9 %copy.35 = bf16[16,8,64,128]{3,2,1,0:T(8,128)(2,1)} copy(bf16[16,8,64,128]{3,1,2,0:T(8,128)(2,1)S(1)} %fusion.4) | data formatting | bytes 4194304
  7.3 0.7 fusion.14
  8.0 4.6 %fusion.102 = (f32[128,2,8]{2,1,0:T(2,128)S(1)}, f32[128,2,8,32]{3,2,1,0:T(8,128)S(1)}) fusion(f32[2,128,128,32]{1,3,0,2:T(8,128)S(1)} %fusion.14, bf16[128,4,2,8,128]{4,3,2,1,0:T(8,128)(2,1)} %bitcast.362, s32[]{:T(128)S(6)} %select_n.72, pred[128,32]{1,0:T(8,128)(4,1)S(1)} %add_compare_fusion), kind=kOutput, calls=%fused_computation.176 | convolution fusion | flops 100857856 | bytes 4993028 | tf_op jit(solution)/shard_map/gstkd,sgkjd->gskjt/dot_general | solution.py:65
  12.6 0.1 select_reduce_fusion.1
  12.8 0.6 reshape.1161
  13.5 0.1 copy.26
  13.6 0.7 convolution_bitcast_fusion
  14.3 0.8 fusion.21
  15.1 3.7 %fusion.5 = f32[128,2,8,128]{3,2,1,0:T(8,128)S(1)} fusion(f32[128,32,2,128]{3,1,0,2:T(8,128)S(1)} %convolution_bitcast_fusion, f32[128,2,8,32]{3,2,1,0:T(8,128)S(1)} %get-tuple-element.30, f32[128,2,8]{2,1,0:T(2,128)S(1)} %copy.26, f32[128,2,8]{2,1,0:T(2,128)S(1)} %get-tuple-element.29, pred[128,32]{1,0:T(8,128)(4,1)S(1)} %add_compare_fusion), kind=kOutput, calls=%fused_computation.9 | convolution fusion | flops 101056512 | bytes 5525504 | tf_op jit(solution)/shard_map/gskjt,gstkd->gskjd/dot_general | solution.py:76
  18.8 0.9 fusion.17
  19.7 0.8 fusion.49
  20.7 0.7 maximum_bitcast_fusion
  21.4 12.7 %all-gather.3 = f32[4,130,128]{2,1,0:T(8,128)S(1)} all-gather(f32[1,130,128]{2,1,0:T(8,128)S(1)} %maximum_bitcast_fusion), channel_id=2, replica_groups=mesh['grp'=4,'seq_0'=4,'seq_1'=4,'seq_2'=2] {'seq_0'}, dimensions={0}, use_global_device_ids=true | all-gather | bytes 332800 | tf_op jit(solution)/shard_map/all_gather | solution.py:19
  34.1 0.2 fusion.39
  34.3 12.9 %all-gather.4 = f32[4,130,128]{2,1,0:T(8,128)S(1)} all-gather(f32[1,130,128]{2,1,0:T(8,128)S(1)} %maximum_bitcast_fusion.1), channel_id=3, replica_groups=mesh['grp'=4,'seq_0'=4,'seq_1'=4,'seq_2'=2] {'seq_1'}, dimensions={0}, use_global_device_ids=true | all-gather | bytes 332800 | tf_op jit(solution)/shard_map/all_gather | solution.py:19
  47.3 0.2 fusion.30
  47.5 1.9 %all-gather.5 = f32[2,130,128]{2,1,0:T(8,128)S(1)} all-gather(f32[1,130,128]{2,1,0:T(8,128)S(1)} %maximum_bitcast_fusion.2), channel_id=4, replica_groups=mesh['grp'=4,'seq_0'=4,'seq_1'=4,'seq_2'=2] {'seq_2'}, dimensions={0}, use_global_device_ids=true | all-gather | bytes 199680 | tf_op jit(solution)/shard_map/all_gather | solution.py:19
  49.8 0.1 add_divide_fusion
  49.9 0.7 stack.2
  50.6 5.3 %all-to-all-start.1 = ((f32[4,1,2,8,8,128]{5,4,3,2,1,0:T(8,128)}), f32[4,1,2,8,8,128]{5,4,3,2,1,0:T(8,128)S(1)}, u32[]{:S(2)}, u32[]{:S(2)}) async-start(f32[4,1,2,8,8,128]{5,4,3,2,1,0:T(8,128)} %stack.2), calls=%async_computation.1 | async-start | bytes 524288 | tf_op jit(solution)/shard_map/all_to_all | solution.py:129
  56.0 0.8 compare_select_fusion.1
  56.7 1.0 scatter_custom_fusion
  57.7 2.0 %gather_fusion = bf16[128,32,256]{2,1,0:T(8,128)(2,1)} fusion(bf16[128,32,256]{2,1,0:T(8,128)(2,1)S(1)} %bitcast.360, s32[1024]{0:T(1024)S(1)} %pad_clamp_fusion), kind=kCustom, calls=%fused_computation | custom fusion | bytes 4194816 | tf_op jit(solution)/shard_map/gather | solution.py:109
  59.7 3.2 %all-to-all-done.1 = f32[4,1,2,8,8,128]{5,4,3,2,1,0:T(8,128)S(1)} async-done(((f32[4,1,2,8,8,128]{5,4,3,2,1,0:T(8,128)}), f32[4,1,2,8,8,128]{5,4,3,2,1,0:T(8,128)S(1)}, u32[]{:S(2)}, u32[]{:S(2)}) %all-to-all-start.1) | async-done | bytes 262176 | tf_op jit(solution)/shard_map/all_to_all | solution.py:129
  62.9 6.9 %all-to-all-start = ((bf16[128,32,256]{2,1,0:T(8,128)(2,1)}), bf16[128,32,256]{2,1,0:T(8,128)(2,1)S(1)}, u32[]{:S(2)}, u32[]{:S(2)}) async-start(bf16[128,32,256]{2,1,0:T(8,128)(2,1)} %gather_fusion), calls=%async_computation | async-start | bytes 4194304 | tf_op jit(solution)/shard_map/all_to_all | solution.py:110
  69.8 30.3 %all-to-all-done = bf16[128,32,256]{2,1,0:T(8,128)(2,1)S(1)} async-done(((bf16[128,32,256]{2,1,0:T(8,128)(2,1)}), bf16[128,32,256]{2,1,0:T(8,128)(2,1)S(1)}, u32[]{:S(2)}, u32[]{:S(2)}) %all-to-all-start) | async-done | bytes 2097184 | tf_op jit(solution)/shard_map/all_to_all | solution.py:110
  100.1 1.3 %copy.52 = bf16[1,4,32,32,256]{4,3,2,1,0:T(8,128)(2,1)} copy(bf16[1,4,32,32,256]{4,3,2,1,0:T(8,128)(2,1)S(1)} %bitcast.361) | data formatting | bytes 4194304
  101.5 0.7 copy.53
  (35 shorter events, 1.0 us)
Async XLA Ops:
  0.7 2.8 %copy-start.2 = (s32[128]{0:T(128)}, s32[128]{0:T(128)S(1)}, u32[]{:S(2)}) copy-start(s32[128]{0:T(128)S(1)} %get-tuple-element.31) | copy-start | bytes 1540
  5.1 2.1 %copy-start = (bf16[1,128,32,256]{3,2,1,0:T(8,128)(2,1)S(1)}, bf16[1,128,32,256]{3,2,1,0:T(8,128)(2,1)}, u32[]{:S(2)}) copy-start(bf16[1,128,32,256]{3,2,1,0:T(8,128)(2,1)} %param.6) | copy-start | bytes 6291460
  13.5 0.9 copy-start.1
  15.1 3.7 %copy-start.3 = (s32[128]{0:T(128)S(1)}, s32[128]{0:T(128)}, u32[]{:S(2)}) copy-start(s32[128]{0:T(128)} %copy-done.2) | copy-start | bytes 1540
  50.6 12.3 %all-to-all-start.1 = ((f32[4,1,2,8,8,128]{5,4,3,2,1,0:T(8,128)}), f32[4,1,2,8,8,128]{5,4,3,2,1,0:T(8,128)S(1)}, u32[]{:S(2)}, u32[]{:S(2)}) async-start(f32[4,1,2,8,8,128]{5,4,3,2,1,0:T(8,128)} %stack.2), calls=%async_computation.1 | async-start | bytes 524288 | tf_op jit(solution)/shard_map/all_to_all | solution.py:129
  62.9 37.2 %all-to-all-start = ((bf16[128,32,256]{2,1,0:T(8,128)(2,1)}), bf16[128,32,256]{2,1,0:T(8,128)(2,1)S(1)}, u32[]{:S(2)}, u32[]{:S(2)}) async-start(bf16[128,32,256]{2,1,0:T(8,128)(2,1)} %gather_fusion), calls=%async_computation | async-start | bytes 4194304 | tf_op jit(solution)/shard_map/all_to_all | solution.py:110
